TPU v7x, 32 devices: a whole 2x2x4 slice. The times are simulated.
32 devices in a mesh: expert: 2 (over x), dp: 16 (over z, y, core).
Axes of the slice: x: 2, y: 2, z: 4, core: 2. Of those that a mesh axis runs over, the one named last changes fastest.
Arguments:
- tokens: bfloat16 [256, 4096], P(('expert', 'dp')), may hold values from -6 to 6
- expert_ids: int32 [256, 2], P(('expert', 'dp')), may hold values from 0 to 1, as said below
- slots: int32 [256, 2], P(('expert', 'dp')), may hold values from -1 to 1, as said below
- mix_weights: float32 [256, 2], P(('expert', 'dp')), may hold values from 0.1 to 1
- w_gate: bfloat16 [2, 4096, 8192], P('expert', None, 'dp'), may hold values from -0.09375 to 0.09375
- w_up: bfloat16 [2, 4096, 8192], P('expert', None, 'dp'), may hold values from -0.09375 to 0.09375
- w_down: bfloat16 [2, 8192, 4096], P('expert', None, 'dp'), may hold values from -0.0625 to 0.0625
Outputs:
- mixed: bfloat16 [256, 4096], P(('expert', 'dp'))
Inputs may be any that keep to these rules, and one draw needn't show every extreme that they name: `expert_ids`: each token names 2 different experts. Within each aligned block of 8 tokens (the tokens of one device), the assignments to one expert get distinct slots among 0 to 1 in some order, at most 2 of them are kept and the others get -1; an expert with 2 or more assignments in the block has all 2 slots used. No two assignments of one block share an expert and a slot. In every block some expert has all 2 slots used.
All inputs are finite; a program needn't handle non-finite values.
Results may differ from a plain program's by a relative error of at most 0.0085.
Values may be sent and summed in bfloat16 or wider, within the bound.
A program may use at most 128 MiB of HBM per device.

v0:
```python
import jax
import jax.numpy as jnp
from jax import lax
from jax.sharding import PartitionSpec as P

CAP = 2


def shards(tokens, expert_ids, slots, mix_weights, w_gate, w_up, w_down):
    tok_rows, model_width = tokens.shape
    experts = lax.axis_size("expert")
    capacity = CAP
    slot_count = experts * capacity
    slot_ids = jnp.arange(slot_count, dtype=jnp.int32)
    slot_expert = slot_ids // capacity
    slot_index = slot_ids % capacity
    matches = (expert_ids[None, :, :] == slot_expert[:, None, None]) & (
        slots[None, :, :] == slot_index[:, None, None]
    )
    occupied = jnp.any(matches, axis=2)
    dispatch_table = occupied.astype(jnp.bfloat16)
    outgoing = jnp.dot(dispatch_table, tokens, preferred_element_type=jnp.float32).astype(
        jnp.bfloat16
    )
    arrived = lax.all_to_all(outgoing, "expert", split_axis=0, concat_axis=0, tiled=True)
    gate_w = w_gate[0]
    up_w = w_up[0]
    down_w = w_down[0]
    portion = lax.all_gather(arrived, "dp", axis=0, tiled=True)
    gate_part = jnp.dot(portion, gate_w, preferred_element_type=jnp.float32)
    up_part = jnp.dot(portion, up_w, preferred_element_type=jnp.float32)
    hidden = (jax.nn.silu(gate_part) * up_part).astype(jnp.bfloat16)
    summed = jnp.dot(
        lax.all_gather(hidden, "dp", axis=1, tiled=True), down_w, preferred_element_type=jnp.float32
    )
    result = summed.astype(jnp.bfloat16)
    groups = lax.axis_size("dp")
    blocks = result.reshape(groups, experts, capacity, result.shape[1])
    blocks = lax.all_to_all(blocks, "expert", split_axis=1, concat_axis=1, tiled=True)
    blocks = lax.all_to_all(blocks, "dp", split_axis=0, concat_axis=3, tiled=True)
    returned = blocks.reshape(slot_count, model_width)
    weight_table = jnp.sum(jnp.where(matches, mix_weights[None, :, :], 0.0), axis=2)
    mixed = jnp.dot(
        weight_table.T,
        returned.astype(jnp.float32),
        precision=lax.Precision.HIGHEST,
        preferred_element_type=jnp.float32,
    )
    return mixed.astype(jnp.bfloat16)


def solution(mesh):
    placed = (
        P(("expert", "dp"), None),
        P(("expert", "dp"), None),
        P(("expert", "dp"), None),
        P(("expert", "dp"), None),
        P("expert", None, "dp"),
        P("expert", None, "dp"),
        P("expert", None, "dp"),
    )
    return jax.shard_map(
        shards, mesh=mesh, in_specs=placed, out_specs=P(("expert", "dp"), None), check_vma=False
    )
```

profile of v0, /device:TPU:0, one launch (start us, length us, event | category | flops | bytes accessed | tf_op | source)
XLA Modules:
  0.0 106.0 jit_solution(6045944678401223639)
XLA Ops:
  6.5 0.0 copy-start
  6.5 0.0 all-gather.3.cloned.1.call-start
  6.5 0.8 fusion.15
  7.4 0.0 copy-done
  7.4 0.1 convolution_convert_fusion.1
  7.6 8.0 %all_to_all.32 = bf16[2,2,4096]{2,1,0:T(2,128)(2,1)S(1)} all-to-all(bf16[2,2,4096]{2,1,0:T(2,128)(2,1)S(1)} %all_to_all.22), channel_id=1, replica_groups=mesh['expert'=2,'dp'=16] {'expert'}, dimensions={0} | all-to-all | bytes 65536 | tf_op jit(solution)/shard_map/all_to_all | solution.py:25
  15.6 23.2 %all-gather = bf16[16,4,4096]{2,1,0:T(4,128)(2,1)S(1)} all-gather(bf16[1,4,4096]{2,1,0:T(4,128)(2,1)S(1)} %reshape.36), channel_id=1, replica_groups=mesh['expert'=2,'dp'=16] {'dp'}, dimensions={0}, use_global_device_ids=true | all-gather | bytes 557056 | tf_op jit(solution)/shard_map/all_gather | solution.py:29
  38.8 0.1 reshape.37
  38.9 0.0 copy-start.1
  38.9 3.2 %fusion.4 = f32[64,512]{1,0:T(8,128)S(1)} fusion(bf16[64,4096]{1,0:T(8,128)(2,1)S(1)} %reshape.37, bf16[1,4096,512]{2,1,0:T(8,128)(2,1)} %param.11), kind=kOutput, calls=%fused_computation.6 | convolution fusion | flops 268435456 | bytes 4849664 | tf_op jit(solution)/shard_map/dot_general | solution.py:30
  42.1 0.3 copy-done.1
  42.3 0.0 copy-start.2
  42.3 1.5 %fusion.9 = bf16[64,512]{1,0:T(8,128)(2,1)} fusion(bf16[64,4096]{1,0:T(8,128)(2,1)S(1)} %reshape.37, bf16[1,4096,512]{2,1,0:T(8,128)(2,1)S(1)} %copy-done.1, f32[64,512]{1,0:T(8,128)S(1)} %fusion.4), kind=kOutput, calls=%fused_computation.9 | convolution fusion | flops 268632064 | bytes 4915200 | tf_op jit(solution)/shard_map/dot_general | solution.py:31
  43.8 0.0 all-gather.3.cloned.1.call-update
  43.8 32.9 %all-gather.3.cloned.1.call-done = bf16[64,8192]{1,0:T(8,128)(2,1)} async-done(((bf16[64,512]{1,0:T(8,128)(2,1)}), bf16[64,8192]{1,0:T(8,128)(2,1)}) %all-gather.3.cloned.1.call-update) | async-done | bytes 1048592 | tf_op jit(solution)/shard_map/all_gather | solution.py:34
  76.8 3.3 %fusion.12 = bf16[64,256]{1,0:T(8,128)(2,1)S(1)} fusion(bf16[64,8192]{1,0:T(8,128)(2,1)} %all-gather.3.cloned.1.call-done, bf16[1,8192,256]{2,1,0:T(8,128)(2,1)} %param.13), kind=kOutput, calls=%fused_computation.10 | convolution fusion | flops 268451840 | bytes 5275648 | tf_op jit(solution)/shard_map/dot_general | solution.py:33
  80.1 6.5 %all_to_all.33 = bf16[16,2,2,256]{3,2,0,1:T(2,128)(2,1)S(1)} all-to-all(bf16[16,2,2,256]{3,2,0,1:T(2,128)(2,1)S(1)} %copy.25), channel_id=1, replica_groups=mesh['expert'=2,'dp'=16] {'expert'}, dimensions={1} | all-to-all | bytes 65536 | tf_op jit(solution)/shard_map/all_to_all | solution.py:39
  86.6 0.6 copy.26
  87.2 4.3 %all-to-all-start.2 = ((bf16[16,2,2,256]{3,2,1,0:T(2,128)(2,1)}), bf16[16,2,2,256]{3,2,1,0:T(2,128)(2,1)S(1)}, u32[]{:S(2)}, u32[]{:S(2)}) async-start(bf16[16,2,2,256]{3,2,1,0:T(2,128)(2,1)} %copy.26), calls=%async_computation.2 | async-start | bytes 65536 | tf_op jit(solution)/shard_map/all_to_all | solution.py:40
  91.6 0.0 copy-done.2
  91.6 6.6 %all-to-all-done.2 = bf16[16,2,2,256]{3,2,1,0:T(2,128)(2,1)S(1)} async-done(((bf16[16,2,2,256]{3,2,1,0:T(2,128)(2,1)}), bf16[16,2,2,256]{3,2,1,0:T(2,128)(2,1)S(1)}, u32[]{:S(2)}, u32[]{:S(2)}) %all-to-all-start.2) | async-done | bytes 32800 | tf_op jit(solution)/shard_map/all_to_all | solution.py:40
  98.2 0.9 convolution_convert_fusion
  (8 shorter events, 0.1 us)
Async XLA Ops:
  6.5 0.8 copy-start
  6.5 70.2 %all-gather.3.cloned.1.call-start = ((), (), s32[]{:S(2)}) async-start(), calls=%async_computation.3 | async-start | bytes 1114112 | tf_op jit(solution)/shard_map/all_gather | solution.py:34
  38.9 3.5 %copy-start.1 = (bf16[1,4096,512]{2,1,0:T(8,128)(2,1)S(1)}, bf16[1,4096,512]{2,1,0:T(8,128)(2,1)}, u32[]{:S(2)}) copy-start(bf16[1,4096,512]{2,1,0:T(8,128)(2,1)} %param.12) | copy-start | bytes 12582916
  42.3 49.2 %copy-start.2 = (f32[8,2]{0,1:T(2,128)S(1)}, f32[8,2]{0,1:T(2,128)}, u32[]{:S(2)}) copy-start(f32[8,2]{0,1:T(2,128)} %param.10) | copy-start | bytes 196
  87.2 11.0 %all-to-all-start.2 = ((bf16[16,2,2,256]{3,2,1,0:T(2,128)(2,1)}), bf16[16,2,2,256]{3,2,1,0:T(2,128)(2,1)S(1)}, u32[]{:S(2)}, u32[]{:S(2)}) async-start(bf16[16,2,2,256]{3,2,1,0:T(2,128)(2,1)} %copy.26), calls=%async_computation.2 | async-start | bytes 65536 | tf_op jit(solution)/shard_map/all_to_all | solution.py:40
Sparse Core Ops, SparseCore 0:
  44.0 32.7 all-gather.2
where the time goes:
time: 106 us
  waiting for transfers between devices  39.5 us (37%)
  blocking collectives  37.7 us (36%)
  between operations  13.5 us (13%)
  matrix products  8.99 us (8%)
  starting transfers between devices  4.33 us (4%)
  local copies, waits for them, and re-layouts  1.17 us (1%)
    all_gather x1, waiting for transfers between devices, shards(): lax.all_gather(hidden, 'dp', axis=1, tiled=True)  32.9 us
    all_gather x1, blocking collectives, shards(): portion = lax.all_gather(arrived, 'dp', axis=0, tiled=True)  23.2 us
    all_to_all x1, blocking collectives, shards(): lax.all_to_all(outgoing, 'expert', split_axis=0, concat_axis=0, tiled=True)  7.98 us
    all_to_all x1, waiting for transfers between devices, shards(): lax.all_to_all(blocks, 'dp', split_axis=0, concat_axis=3, tiled=True)  6.61 us
    all_to_all x1, blocking collectives, shards(): lax.all_to_all(blocks, 'expert', split_axis=1, concat_axis=1, tiled=True)  6.47 us
    all_to_all x1, starting transfers between devices, shards(): lax.all_to_all(blocks, 'dp', split_axis=0, concat_axis=3, tiled=True)  4.33 us
    dot_general x1, matrix products, shards(): jnp.dot(lax.all_gather(hidden, 'dp', axis=1, tiled=True), down_w, preferr...  3.31 us
    dot_general x1, matrix products, shards(): gate_part = jnp.dot(portion, gate_w, preferred_element_type=jnp.float32)  3.18 us
  transfers between devices with their start and end apart: 2, of which 2 were waited for; matrix products, arithmetic and copies ran while one was open for 0% of the time, Pallas kernels for 0%

commit v1 on v0

--- a/solution.py
+++ b/solution.py
@@ -4,6 +4,15 @@
 from jax.sharding import PartitionSpec as P
 
 CAP = 2
+
+
+def _attach_stops_all(body):
+    current_block = lax.axis_size("dp")
+    work_now = jnp.split(body, current_block, 0)
+    x_now = jnp.stack(work_now, 0)
+    new = lax.all_to_all(x_now, axis_name="dp", split_axis=0, concat_axis=0)
+    e_now = jnp.concatenate(new, 3)
+    return e_now
 
 
 def shards(tokens, expert_ids, slots, mix_weights, w_gate, w_up, w_down):
@@ -37,7 +46,7 @@
     groups = lax.axis_size("dp")
     blocks = result.reshape(groups, experts, capacity, result.shape[1])
     blocks = lax.all_to_all(blocks, "expert", split_axis=1, concat_axis=1, tiled=True)
-    blocks = lax.all_to_all(blocks, "dp", split_axis=0, concat_axis=3, tiled=True)
+    blocks = _attach_stops_all(blocks)
     returned = blocks.reshape(slot_count, model_width)
     weight_table = jnp.sum(jnp.where(matches, mix_weights[None, :, :], 0.0), axis=2)
     mixed = jnp.dot(

time: 106 us -> 115 us (1.085)
  local copies, waits for them, and re-layouts: 1.17 us -> 9.83 us
    unnamed x9 -> x24, local copies, waits for them, and re-layouts: 0.45 us -> 9.17 us
where the time goes in v1:
time: 115 us
  waiting for transfers between devices  39.5 us (34%)
  blocking collectives  37.7 us (33%)
  between operations  13.5 us (12%)
  local copies, waits for them, and re-layouts  9.83 us (9%)
  matrix products  8.98 us (8%)
  starting transfers between devices  4.33 us (4%)
    all_gather x1, waiting for transfers between devices, shards(): lax.all_gather(hidden, 'dp', axis=1, tiled=True)  32.9 us
    all_gather x1, blocking collectives, shards(): portion = lax.all_gather(arrived, 'dp', axis=0, tiled=True)  23.2 us
    unnamed x24, local copies, waits for them, and re-layouts  9.17 us
    all_to_all x1, blocking collectives, shards(): lax.all_to_all(outgoing, 'expert', split_axis=0, concat_axis=0, tiled=True)  7.98 us
    all_to_all x1, waiting for transfers between devices, _attach_stops_all(): new = lax.all_to_all(x_now, axis_name='dp', split_axis=0, concat_axis=0)  6.61 us
    all_to_all x1, blocking collectives, shards(): lax.all_to_all(blocks, 'expert', split_axis=1, concat_axis=1, tiled=True)  6.47 us
    all_to_all x1, starting transfers between devices, _attach_stops_all(): new = lax.all_to_all(x_now, axis_name='dp', split_axis=0, concat_axis=0)  4.33 us
    dot_general x1, matrix products, shards(): jnp.dot(lax.all_gather(hidden, 'dp', axis=1, tiled=True), down_w, preferr...  3.31 us
  transfers between devices with their start and end apart: 2, of which 2 were waited for; matrix products, arithmetic and copies ran while one was open for 0% of the time, Pallas kernels for 0%

profile of v1, /device:TPU:0, one launch (start us, length us, event | category | flops | bytes accessed | tf_op | source)
XLA Modules:
  0.0 114.6 jit_solution(16671751464143794837)
XLA Ops:
  6.5 0.8 fusion.15
  7.4 0.0 copy-done
  7.4 0.1 convolution_convert_fusion.1
  7.6 8.0 %all_to_all.22 = bf16[2,2,4096]{2,1,0:T(2,128)(2,1)S(1)} all-to-all(bf16[2,2,4096]{2,1,0:T(2,128)(2,1)S(1)} %all_to_all.14), channel_id=1, replica_groups=mesh['expert'=2,'dp'=16] {'expert'}, dimensions={0} | all-to-all | bytes 65536 | tf_op jit(solution)/shard_map/all_to_all | solution.py:34
  15.6 23.2 %all-gather = bf16[16,4,4096]{2,1,0:T(4,128)(2,1)S(1)} all-gather(bf16[1,4,4096]{2,1,0:T(4,128)(2,1)S(1)} %reshape.35), channel_id=1, replica_groups=mesh['expert'=2,'dp'=16] {'dp'}, dimensions={0}, use_global_device_ids=true | all-gather | bytes 557056 | tf_op jit(solution)/shard_map/all_gather | solution.py:38
  38.8 0.1 reshape.36
  38.9 3.2 %fusion.4 = f32[64,512]{1,0:T(8,128)S(1)} fusion(bf16[64,4096]{1,0:T(8,128)(2,1)S(1)} %reshape.36, bf16[1,4096,512]{2,1,0:T(8,128)(2,1)} %param.11), kind=kOutput, calls=%fused_computation.6 | convolution fusion | flops 268435456 | bytes 4849664 | tf_op jit(solution)/shard_map/dot_general | solution.py:39
  42.1 0.3 copy-done.1
  42.3 1.5 %fusion.9 = bf16[64,512]{1,0:T(8,128)(2,1)} fusion(bf16[64,4096]{1,0:T(8,128)(2,1)S(1)} %reshape.36, bf16[1,4096,512]{2,1,0:T(8,128)(2,1)S(1)} %copy-done.1, f32[64,512]{1,0:T(8,128)S(1)} %fusion.4), kind=kOutput, calls=%fused_computation.9 | convolution fusion | flops 268632064 | bytes 4915200 | tf_op jit(solution)/shard_map/dot_general | solution.py:40
  43.8 0.0 all-gather.3.cloned.1.call-update
  43.8 32.9 %all-gather.3.cloned.1.call-done = bf16[64,8192]{1,0:T(8,128)(2,1)} async-done(((bf16[64,512]{1,0:T(8,128)(2,1)}), bf16[64,8192]{1,0:T(8,128)(2,1)}) %all-gather.3.cloned.1.call-update) | async-done | bytes 1048592 | tf_op jit(solution)/shard_map/all_gather | solution.py:43
  76.8 3.3 %fusion.12 = bf16[64,256]{1,0:T(8,128)(2,1)S(1)} fusion(bf16[64,8192]{1,0:T(8,128)(2,1)} %all-gather.3.cloned.1.call-done, bf16[1,8192,256]{2,1,0:T(8,128)(2,1)} %param.13), kind=kOutput, calls=%fused_computation.10 | convolution fusion | flops 268451840 | bytes 5275648 | tf_op jit(solution)/shard_map/dot_general | solution.py:42
  80.1 6.5 %all_to_all.23 = bf16[16,2,2,256]{3,2,0,1:T(2,128)(2,1)S(1)} all-to-all(bf16[16,2,2,256]{3,2,0,1:T(2,128)(2,1)S(1)} %copy.53), channel_id=1, replica_groups=mesh['expert'=2,'dp'=16] {'expert'}, dimensions={1} | all-to-all | bytes 65536 | tf_op jit(solution)/shard_map/all_to_all | solution.py:48
  86.6 0.6 constant_dynamic-update-slice_fusion.15
  87.2 0.6 constant_dynamic-update-slice_fusion.14
  87.8 0.6 constant_dynamic-update-slice_fusion.13
  88.3 0.6 constant_dynamic-update-slice_fusion.12
  88.9 0.6 constant_dynamic-update-slice_fusion.11
  89.5 0.6 constant_dynamic-update-slice_fusion.10
  90.1 0.6 constant_dynamic-update-slice_fusion.9
  90.7 0.6 constant_dynamic-update-slice_fusion.8
  91.2 0.6 constant_dynamic-update-slice_fusion.7
  91.8 0.6 constant_dynamic-update-slice_fusion.6
  92.4 0.6 constant_dynamic-update-slice_fusion.5
  93.0 0.6 constant_dynamic-update-slice_fusion.4
  93.6 0.6 constant_dynamic-update-slice_fusion.3
  94.2 0.6 constant_dynamic-update-slice_fusion.2
  94.7 0.6 constant_dynamic-update-slice_fusion.1
  95.3 0.6 constant_dynamic-update-slice_fusion
  95.9 4.3 %all-to-all-start.2 = ((bf16[16,1,2,2,256]{4,3,2,1,0:T(2,128)(2,1)}), bf16[16,1,2,2,256]{4,3,2,1,0:T(2,128)(2,1)S(1)}, u32[]{:S(2)}, u32[]{:S(2)}) async-start(bf16[16,1,2,2,256]{4,3,2,1,0:T(2,128)(2,1)} %constant_dynamic-update-slice_fusion), calls=%async_computation.2 | async-start | bytes 65536 | tf_op jit(solution)/shard_map/all_to_all | solution.py:13
  100.3 6.6 %all-to-all-done.2 = bf16[16,1,2,2,256]{4,3,2,1,0:T(2,128)(2,1)S(1)} async-done(((bf16[16,1,2,2,256]{4,3,2,1,0:T(2,128)(2,1)}), bf16[16,1,2,2,256]{4,3,2,1,0:T(2,128)(2,1)S(1)}, u32[]{:S(2)}, u32[]{:S(2)}) %all-to-all-start.2) | async-done | bytes 32800 | tf_op jit(solution)/shard_map/all_to_all | solution.py:13
  106.9 0.9 convolution_convert_fusion
  (13 shorter events, 0.1 us)
Async XLA Ops:
  6.5 0.8 copy-start
  6.5 70.2 %all-gather.3.cloned.1.call-start = ((), (), s32[]{:S(2)}) async-start(), calls=%async_computation.3 | async-start | bytes 1114112 | tf_op jit(solution)/shard_map/all_gather | solution.py:43
  38.9 3.5 %copy-start.1 = (bf16[1,4096,512]{2,1,0:T(8,128)(2,1)S(1)}, bf16[1,4096,512]{2,1,0:T(8,128)(2,1)}, u32[]{:S(2)}) copy-start(bf16[1,4096,512]{2,1,0:T(8,128)(2,1)} %param.12) | copy-start | bytes 12582916
  42.3 57.9 %copy-start.2 = (f32[8,2]{0,1:T(2,128)S(1)}, f32[8,2]{0,1:T(2,128)}, u32[]{:S(2)}) copy-start(f32[8,2]{0,1:T(2,128)} %param.10) | copy-start | bytes 196
  95.9 11.0 %all-to-all-start.2 = ((bf16[16,1,2,2,256]{4,3,2,1,0:T(2,128)(2,1)}), bf16[16,1,2,2,256]{4,3,2,1,0:T(2,128)(2,1)S(1)}, u32[]{:S(2)}, u32[]{:S(2)}) async-start(bf16[16,1,2,2,256]{4,3,2,1,0:T(2,128)(2,1)} %constant_dynamic-update-slice_fusion), calls=%async_computation.2 | async-start | bytes 65536 | tf_op jit(solution)/shard_map/all_to_all | solution.py:13
Sparse Core Ops, SparseCore 0:
  44.0 32.7 all-gather.2
